TPU v7x, 32 devices: a whole 2x2x4 slice. The times are simulated.
32 devices in a mesh: row: 4 (over z), col: 4 (over y, x), layer: 2 (over core).
Axes of the slice: x: 2, y: 2, z: 4, core: 2. Of those that a mesh axis runs over, the one named last changes fastest.
Arguments:
- wavefunction: float32 [4096, 4096], P('row', 'col'), may hold values from -0.015625 to 1.515625
- start_block: float32 [4096, 2048], P(('col', 'layer'), 'row'), may hold values from -6 to 6
Outputs:
- basis: float32 [4096, 2048], P(('col', 'layer'), 'row')
All inputs are finite; a program needn't handle non-finite values.
Results may differ from a plain program's by a relative error of at most 0.0003.
Values sent between devices are 32-bit elements; how exact they have to be, the bound alone decides.
No kernel may reach another device: no remote copies, remote signals or barrier semaphores. Data moves between devices by JAX's collectives and lax.ppermute only.
A program may use at most 128 MiB of HBM per device.

v0:
```python
import math
import jax
import jax.numpy as jnp
from jax import lax
from jax.sharding import PartitionSpec as P


def spread(x, axis, root):
    mine = lax.axis_index(axis) == root
    return lax.psum(jnp.where(mine, x, jnp.zeros_like(x)), axis)


def cross(left, right):
    return lax.dot_general(
        left,
        right,
        (((0,), (0,)), ((), ())),
        precision=lax.Precision.HIGHEST,
        preferred_element_type=jnp.float32,
    )


def times(left, right):
    return jnp.dot(left, right, precision=lax.Precision.HIGHEST, preferred_element_type=jnp.float32)


def apply_density(rho_slab, basis_block):
    return lax.psum_scatter(
        cross(rho_slab, basis_block), ("col", "layer"), scatter_dimension=0, tiled=True
    )


def orthonormalize(image_block):
    panel_owner = lax.axis_index("row")
    panels = lax.axis_size("row")
    current = image_block
    gram_matrix = lax.psum(cross(current, current), ("col", "layer"))
    for panel_index in range(panels):
        factor = jnp.linalg.cholesky(gram_matrix)
        new_basis = jax.scipy.linalg.solve_triangular(factor, current.T, lower=True).T
        current = jnp.where(panel_owner == panel_index, new_basis, current)
        if panel_index + 1 < panels:
            chosen = spread(current, "row", panel_index)
            later = panel_owner > panel_index
            correlation, square = lax.psum(
                (cross(chosen, current), cross(current, current)), ("col", "layer")
            )
            current = jnp.where(later, current - times(chosen, correlation), current)
            gram_matrix = jnp.where(later, square - cross(correlation, correlation), square)
    return current


def shards(wavefunction, start_block):
    layers = lax.axis_size("layer")
    column_width = wavefunction.shape[1] // layers
    own_slice = lax.dynamic_slice_in_dim(
        wavefunction, lax.axis_index("layer") * column_width, column_width, 1
    )
    own_rows = lax.all_gather(own_slice, "col", axis=1, tiled=True)
    partner = spread(own_rows, "row", lax.axis_index("col"))
    rho_part = lax.psum_scatter(
        lax.dot_general(
            partner,
            own_rows,
            (((1,), (1,)), ((), ())),
            precision=lax.Precision.HIGHEST,
            preferred_element_type=jnp.float32,
        ),
        "layer",
        scatter_dimension=0,
        tiled=True,
    )
    rho_slab = lax.all_gather(rho_part, "row", axis=1, tiled=True)
    current = start_block
    image_block = apply_density(rho_slab, current)
    current = orthonormalize(image_block)
    return current * math.sqrt(rho_slab.shape[1])


def solution(mesh):
    placed = (P("row", "col"), P(("col", "layer"), "row"))
    return jax.shard_map(
        shards, mesh=mesh, in_specs=placed, out_specs=P(("col", "layer"), "row"), check_vma=False
    )
```

profile of v0, /device:TPU:0, one launch (start us, length us, event | category | flops | bytes accessed | tf_op | source)
XLA Modules:
  0.0 1721.6 jit_solution(5460350467099761118)
XLA Ops:
  9.9 90.3 %all-gather.3.cloned.1.call-done = f32[1024,2048]{1,0:T(8,128)} async-done(((f32[1024,512]{1,0:T(8,128)}), f32[1024,2048]{1,0:T(8,128)}) %all-gather.3.cloned.1.call-update) | async-done | bytes 8388624 | tf_op jit(solution)/shard_map/all_gather | solution.py:59
  108.5 290.9 %all-reduce.13.cloned.1.call-done = f32[1024,2048]{1,0:T(8,128)} async-done(((f32[1024,2048]{1,0:T(8,128)}), f32[1024,2048]{1,0:T(8,128)}) %all-reduce.13.cloned.1.call-update) | async-done | bytes 8388624 | tf_op jit(solution)/shard_map/psum | solution.py:10
  399.4 32.1 %fusion.156 = f32[1024,1024]{1,0:T(8,128)} fusion(f32[1024,2048]{1,0:T(8,128)} %all-reduce.13.cloned.1.call-done, f32[1024,2048]{1,0:T(8,128)} %all-gather.3.cloned.1.call-done), kind=kOutput, calls=%fused_computation.284 | convolution fusion | flops 25769803776 | bytes 20971520 | tf_op jit(solution)/shard_map/dot_general | solution.py:62
  443.1 152.0 %all-gather.5.cloned.1.call-done = f32[512,4096]{1,0:T(8,128)} async-done(((f32[512,1024]{1,0:T(8,128)}), f32[512,4096]{1,0:T(8,128)}) %all-gather.5.cloned.1.call-update) | async-done | bytes 8388624 | tf_op jit(solution)/shard_map/all_gather | solution.py:73
  595.1 17.1 fusion.157
  612.2 69.6 %reduce-scatter.5.cloned.1.call-done = f32[512,512]{0,1:T(8,128)} async-done(((f32[4096,512]{0,1:T(8,128)}), f32[512,512]{0,1:T(8,128)}) %reduce-scatter.5.cloned.1.call-update) | async-done | bytes 1048592 | tf_op jit(solution)/shard_map/reduce_scatter | solution.py:28
  686.9 56.3 %all-reduce.15.cloned.1.call-done = f32[512,512]{0,1:T(8,128)} async-done(((f32[512,512]{0,1:T(8,128)}), f32[512,512]{0,1:T(8,128)}) %all-reduce.15.cloned.1.call-update) | async-done | bytes 1048592 | tf_op jit(solution)/shard_map/psum | solution.py:37
  746.2 11.7 cholesky.462
  768.6 11.7 cholesky.481
  790.9 11.7 cholesky.502
  813.8 11.7 cholesky.519
  838.3 39.3 %custom-call.38 = f32[4,128,128]{1,2,0:T(8,128)S(1)} custom-call(f32[4,128,128]{2,1,0:T(8,128)S(1)} %get-tuple-element.33), custom_call_target="InvertDiagBlocksLowerTriangular" | custom-call | tf_op jit(solution)/shard_map/jit(_solve_triangular)/triangular_solve | solution.py:40
  884.9 48.4 %all-reduce.17.cloned.1.call-done = f32[512,512]{0,1:T(8,128)} async-done(((f32[512,512]{0,1:T(8,128)}), f32[512,512]{0,1:T(8,128)}) %all-reduce.17.cloned.1.call-update) | async-done | bytes 1048592 | tf_op jit(solution)/shard_map/psum | solution.py:10
  937.8 60.8 %all-reduce.27.cloned.1.call-done = (f32[512,512]{1,0:T(8,128)}, f32[512,512]{0,1:T(8,128)}) async-done(((f32[512,512]{1,0:T(8,128)}, f32[512,512]{0,1:T(8,128)}), (f32[512,512]{1,0:T(8,128)}, f32[512,512]{0,1:T(8,128)})) %all-reduce.27.cloned.1.call-update) | async-done | bytes 2097168 | tf_op jit(solution)/shard_map/psum | solution.py:45
  1006.3 11.7 cholesky.534
  1030.6 11.9 cholesky.553
  1055.2 11.7 cholesky.574
  1078.8 12.1 cholesky.591
  1106.6 39.3 %custom-call.42 = f32[4,128,128]{1,2,0:T(8,128)S(1)} custom-call(f32[4,128,128]{2,1,0:T(8,128)S(1)} %get-tuple-element.34), custom_call_target="InvertDiagBlocksLowerTriangular" | custom-call | tf_op jit(solution)/shard_map/jit(_solve_triangular)/triangular_solve | solution.py:40
  1159.0 48.2 %all-reduce.19.cloned.1.call-done = f32[512,512]{0,1:T(8,128)} async-done(((f32[512,512]{0,1:T(8,128)}), f32[512,512]{0,1:T(8,128)}) %all-reduce.19.cloned.1.call-update) | async-done | bytes 1048592 | tf_op jit(solution)/shard_map/psum | solution.py:10
  1211.5 61.1 %all-reduce.25.cloned.1.call-done = (f32[512,512]{1,0:T(8,128)}, f32[512,512]{0,1:T(8,128)}) async-done(((f32[512,512]{1,0:T(8,128)}, f32[512,512]{0,1:T(8,128)}), (f32[512,512]{1,0:T(8,128)}, f32[512,512]{0,1:T(8,128)})) %all-reduce.25.cloned.1.call-update) | async-done | bytes 2097168 | tf_op jit(solution)/shard_map/psum | solution.py:45
  1280.2 11.7 cholesky.606
  1304.5 11.9 cholesky.625
  1329.1 11.7 cholesky.646
  1352.8 12.1 cholesky.663
  1380.5 39.3 %custom-call.46 = f32[4,128,128]{1,2,0:T(8,128)S(1)} custom-call(f32[4,128,128]{2,1,0:T(8,128)S(1)} %get-tuple-element.35), custom_call_target="InvertDiagBlocksLowerTriangular" | custom-call | tf_op jit(solution)/shard_map/jit(_solve_triangular)/triangular_solve | solution.py:40
  1433.1 48.0 %all-reduce.21.cloned.1.call-done = f32[512,512]{0,1:T(8,128)} async-done(((f32[512,512]{0,1:T(8,128)}), f32[512,512]{0,1:T(8,128)}) %all-reduce.21.cloned.1.call-update) | async-done | bytes 1048592 | tf_op jit(solution)/shard_map/psum | solution.py:10
  1485.2 61.3 %all-reduce.23.cloned.1.call-done = (f32[512,512]{1,0:T(8,128)}, f32[512,512]{0,1:T(8,128)}) async-done(((f32[512,512]{1,0:T(8,128)}, f32[512,512]{0,1:T(8,128)}), (f32[512,512]{1,0:T(8,128)}, f32[512,512]{0,1:T(8,128)})) %all-reduce.23.cloned.1.call-update) | async-done | bytes 2097168 | tf_op jit(solution)/shard_map/psum | solution.py:45
  1554.2 11.7 cholesky.678
  1631.5 11.7 cholesky.735
  1650.2 13.7 while.11
  1663.9 40.1 %custom-call.50 = f32[4,128,128]{1,2,0:T(8,128)S(1)} custom-call(f32[4,128,128]{2,1,0:T(8,128)} %get-tuple-element.36), custom_call_target="InvertDiagBlocksLowerTriangular" | custom-call | tf_op jit(solution)/shard_map/jit(_solve_triangular)/triangular_solve | solution.py:40
  (245 shorter events, 368.6 us)
Async XLA Ops:
  6.5 588.5 %copy-start = (f32[512,512]{1,0:T(8,128)S(1)}, f32[512,512]{1,0:T(8,128)}, u32[]{:S(2)}) copy-start(f32[512,512]{1,0:T(8,128)} %param.6) | copy-start | bytes 3145732
  6.5 93.6 %all-gather.3.cloned.1.call-start = ((), (), s32[]{:S(2)}) async-start(), calls=%async_computation.2 | async-start | bytes 10485760 | tf_op jit(solution)/shard_map/all_gather | solution.py:59
  9.8 389.6 %all-reduce.13.cloned.1.call-start = ((), (), s32[]{:S(2)}) async-start(), calls=%async_computation.3 | async-start | bytes 16777216 | tf_op jit(solution)/shard_map/psum | solution.py:10
  108.4 334.3 %reduce-scatter.3.cloned.1.call-start = ((), (), s32[]{:S(2)}) async-start(), calls=%async_computation.4 | async-start | bytes 6291456 | tf_op jit(solution)/shard_map/reduce_scatter | solution.py:61
  431.5 163.5 %all-gather.5.cloned.1.call-start = ((), (), s32[]{:S(2)}) async-start(), calls=%async_computation.5 | async-start | bytes 10485760 | tf_op jit(solution)/shard_map/all_gather | solution.py:73
  442.7 239.1 %reduce-scatter.5.cloned.1.call-start = ((), (), s32[]{:S(2)}) async-start(), calls=%async_computation.6 | async-start | bytes 9437184 | tf_op jit(solution)/shard_map/reduce_scatter | solution.py:28
  612.2 131.0 %all-reduce.15.cloned.1.call-start = ((), (), s32[]{:S(2)}) async-start(), calls=%async_computation.7 | async-start | bytes 2097152 | tf_op jit(solution)/shard_map/psum | solution.py:37
  681.8 195.8 %copy-start.2 = (f32[512,512]{0,1:T(8,128)S(1)}, f32[512,512]{0,1:T(8,128)}, u32[]{:S(2)}) copy-start(f32[512,512]{0,1:T(8,128)} %reduce-scatter.5.cloned.1.call-done) | copy-start | bytes 3145732
  686.3 247.0 %all-reduce.17.cloned.1.call-start = ((), (), s32[]{:S(2)}) async-start(), calls=%async_computation.8 | async-start | bytes 2097152 | tf_op jit(solution)/shard_map/psum | solution.py:10
  882.0 116.7 %all-reduce.27.cloned.1.call-start = ((), (), s32[]{:S(2)}) async-start(), calls=%async_computation.13 | async-start | bytes 4194304 | tf_op jit(solution)/shard_map/psum | solution.py:45
  937.4 269.8 %all-reduce.19.cloned.1.call-start = ((), (), s32[]{:S(2)}) async-start(), calls=%async_computation.9 | async-start | bytes 2097152 | tf_op jit(solution)/shard_map/psum | solution.py:10
  998.7 147.3 %copy-start.4 = (f32[512,512]{1,0:T(8,128)S(1)}, f32[512,512]{1,0:T(8,128)}, u32[]{:S(2)}) copy-start(f32[512,512]{1,0:T(8,128)} %get-tuple-element.73) | copy-start | bytes 3145732
  1005.4 1.0 copy-start.6
  1156.1 116.5 %all-reduce.25.cloned.1.call-start = ((), (), s32[]{:S(2)}) async-start(), calls=%async_computation.12 | async-start | bytes 4194304 | tf_op jit(solution)/shard_map/psum | solution.py:45
  1211.3 269.9 %all-reduce.21.cloned.1.call-start = ((), (), s32[]{:S(2)}) async-start(), calls=%async_computation.10 | async-start | bytes 2097152 | tf_op jit(solution)/shard_map/psum | solution.py:10
  1272.6 147.3 %copy-start.5 = (f32[512,512]{1,0:T(8,128)S(1)}, f32[512,512]{1,0:T(8,128)}, u32[]{:S(2)}) copy-start(f32[512,512]{1,0:T(8,128)} %get-tuple-element.71) | copy-start | bytes 3145732
  1279.3 1.0 copy-start.7
  1430.1 116.5 %all-reduce.23.cloned.1.call-start = ((), (), s32[]{:S(2)}) async-start(), calls=%async_computation.11 | async-start | bytes 4194304 | tf_op jit(solution)/shard_map/psum | solution.py:45
  1546.5 157.5 %copy-start.3 = (f32[512,512]{1,0:T(8,128)S(1)}, f32[512,512]{1,0:T(8,128)}, u32[]{:S(2)}) copy-start(f32[512,512]{1,0:T(8,128)} %get-tuple-element.69) | copy-start | bytes 3145732
  1553.2 1.0 copy-start.8
  1647.0 67.5 %copy-start.1 = (f32[512,512]{1,0:T(8,128)S(1)}, f32[512,512]{1,0:T(8,128)}, u32[]{:S(2)}) copy-start(f32[512,512]{1,0:T(8,128)} %param.6) | copy-start | bytes 3145732
Sparse Core Ops, SparseCore 0:
  9.9 90.1 all-gather.2
  108.5 290.8 all-reduce.12
  431.7 10.9 reduce-scatter.2
  444.1 150.8 all-gather.4
  612.3 69.4 reduce-scatter.4
  686.4 56.6 all-reduce.14
  882.1 51.1 all-reduce.16
  937.5 61.1 all-reduce.26
  1156.2 50.9 all-reduce.18
  1211.4 61.1 all-reduce.24
  1430.2 50.9 all-reduce.20
  1485.3 61.1 all-reduce.22
where the time goes:
time: 1730 us; the launch traced here: 1720 us
  waiting for transfers between devices  998 us (58%)
  other arithmetic  500 us (29%)
  matrix products  136 us (8%)
  local copies, waits for them, and re-layouts  59.8 us (3%)
  between operations  24.6 us (1%)
    psum x4, waiting for transfers between devices, spread(): return lax.psum(jnp.where(mine, x, jnp.zeros_like(x)), axis)  436 us
    another operation x59, other arithmetic, orthonormalize(): factor = jnp.linalg.cholesky(gram_matrix)  319 us
    psum x3, waiting for transfers between devices, orthonormalize(): lax.psum((cross(chosen, current), cross(current, current)), ('col', 'laye...  183 us
    another operation x9, other arithmetic, orthonormalize(): jax.scipy.linalg.solve_triangular(factor, current.T, lower=True)  163 us
    all_gather x1, waiting for transfers between devices, shards(): rho_slab = lax.all_gather(rho_part, 'row', axis=1, tiled=True)  152 us
    all_gather x1, waiting for transfers between devices, shards(): own_rows = lax.all_gather(own_slice, 'col', axis=1, tiled=True)  90.3 us
    reduce_scatter x1, waiting for transfers between devices, apply_density(): lax.psum_scatter(cross(rho_slab, basis_block), ('col', 'layer'), scatter_...  69.6 us
    psum x1, waiting for transfers between devices, orthonormalize(): gram_matrix = lax.psum(cross(current, current), ('col', 'layer'))  56.3 us
  transfers between devices with their start and end apart: 12, of which 12 were waited for; matrix products, arithmetic and copies ran while one was open for 0% of the time, Pallas kernels for 0%

commit v1 on v0

--- a/solution.py
+++ b/solution.py
@@ -42,8 +42,14 @@
         if panel_index + 1 < panels:
             chosen = spread(current, "row", panel_index)
             later = panel_owner > panel_index
-            correlation, square = lax.psum(
-                (cross(chosen, current), cross(current, current)), ("col", "layer")
+
+            def post_surface_in(view, group_axis, row_axis):
+                for rr in (group_axis, row_axis):
+                    view = lax.psum(view, axis_name=rr)
+                return view
+
+            correlation, square = post_surface_in(
+                (cross(chosen, current), cross(current, current)), "layer", "col"
             )
             current = jnp.where(later, current - times(chosen, correlation), current)
             gram_matrix = jnp.where(later, square - cross(correlation, correlation), square)

time: 1730 us -> 1830 us (1.058)
  waiting for transfers between devices: 998 us -> 1100 us
    psum x3 -> x6, waiting for transfers between devices: 183 us -> 282 us  [post_surface_in(): view = lax.psum(view, axis_name=rr)]
  transfers between devices with their start and end apart: 12 -> 15, of which waited for: 12 -> 15; matrix products, arithmetic and copies ran while one was open for 0% -> 0% of each run, Pallas kernels for 0% -> 0%
where the time goes in v1:
time: 1830 us; the launch traced here: 1820 us
  waiting for transfers between devices  1100 us (60%)
  other arithmetic  500 us (27%)
  matrix products  137 us (7%)
  local copies, waits for them, and re-layouts  59.8 us (3%)
  between operations  24.6 us (1%)
    psum x4, waiting for transfers between devices, spread(): return lax.psum(jnp.where(mine, x, jnp.zeros_like(x)), axis)  437 us
    another operation x59, other arithmetic, orthonormalize(): factor = jnp.linalg.cholesky(gram_matrix)  319 us
    psum x6, waiting for transfers between devices, post_surface_in(): view = lax.psum(view, axis_name=rr)  282 us
    another operation x9, other arithmetic, orthonormalize(): jax.scipy.linalg.solve_triangular(factor, current.T, lower=True)  163 us
    all_gather x1, waiting for transfers between devices, shards(): rho_slab = lax.all_gather(rho_part, 'row', axis=1, tiled=True)  152 us
    all_gather x1, waiting for transfers between devices, shards(): own_rows = lax.all_gather(own_slice, 'col', axis=1, tiled=True)  90.3 us
    reduce_scatter x1, waiting for transfers between devices, apply_density(): lax.psum_scatter(cross(rho_slab, basis_block), ('col', 'layer'), scatter_...  69.6 us
    psum x1, waiting for transfers between devices, orthonormalize(): gram_matrix = lax.psum(cross(current, current), ('col', 'layer'))  56.6 us
  transfers between devices with their start and end apart: 15, of which 15 were waited for; matrix products, arithmetic and copies ran while one was open for 0% of the time, Pallas kernels for 0%

profile of v1, /device:TPU:0, one launch (start us, length us, event | category | flops | bytes accessed | tf_op | source)
XLA Modules:
  0.0 1823.1 jit_solution(13976838146233625954)
XLA Ops:
  9.9 90.3 %all-gather.3.cloned.1.call-done = f32[1024,2048]{1,0:T(8,128)} async-done(((f32[1024,512]{1,0:T(8,128)}), f32[1024,2048]{1,0:T(8,128)}) %all-gather.3.cloned.1.call-update) | async-done | bytes 8388624 | tf_op jit(solution)/shard_map/all_gather | solution.py:65
  108.5 290.9 %all-reduce.19.cloned.1.call-done = f32[1024,2048]{1,0:T(8,128)} async-done(((f32[1024,2048]{1,0:T(8,128)}), f32[1024,2048]{1,0:T(8,128)}) %all-reduce.19.cloned.1.call-update) | async-done | bytes 8388624 | tf_op jit(solution)/shard_map/psum | solution.py:10
  399.4 32.1 %fusion.156 = f32[1024,1024]{1,0:T(8,128)} fusion(f32[1024,2048]{1,0:T(8,128)} %all-reduce.19.cloned.1.call-done, f32[1024,2048]{1,0:T(8,128)} %all-gather.3.cloned.1.call-done), kind=kOutput, calls=%fused_computation.284 | convolution fusion | flops 25769803776 | bytes 20971520 | tf_op jit(solution)/shard_map/dot_general | solution.py:68
  443.0 152.1 %all-gather.5.cloned.1.call-done = f32[512,4096]{1,0:T(8,128)} async-done(((f32[512,1024]{1,0:T(8,128)}), f32[512,4096]{1,0:T(8,128)}) %all-gather.5.cloned.1.call-update) | async-done | bytes 8388624 | tf_op jit(solution)/shard_map/all_gather | solution.py:79
  595.1 17.1 fusion.157
  612.2 69.6 %reduce-scatter.5.cloned.1.call-done = f32[512,512]{0,1:T(8,128)} async-done(((f32[4096,512]{0,1:T(8,128)}), f32[512,512]{0,1:T(8,128)}) %reduce-scatter.5.cloned.1.call-update) | async-done | bytes 1048592 | tf_op jit(solution)/shard_map/reduce_scatter | solution.py:28
  686.6 56.6 %all-reduce.21.cloned.1.call-done = f32[512,512]{0,1:T(8,128)} async-done(((f32[512,512]{0,1:T(8,128)}), f32[512,512]{0,1:T(8,128)}) %all-reduce.21.cloned.1.call-update) | async-done | bytes 1048592 | tf_op jit(solution)/shard_map/psum | solution.py:37
  746.2 11.7 cholesky.462
  768.6 11.7 cholesky.481
  791.2 11.7 cholesky.502
  814.1 11.7 cholesky.519
  838.5 39.3 %custom-call.38 = f32[4,128,128]{1,2,0:T(8,128)S(1)} custom-call(f32[4,128,128]{2,1,0:T(8,128)S(1)} %get-tuple-element.33), custom_call_target="InvertDiagBlocksLowerTriangular" | custom-call | tf_op jit(solution)/shard_map/jit(_solve_triangular)/triangular_solve | solution.py:40
  885.2 48.3 %all-reduce.23.cloned.1.call-done = f32[512,512]{0,1:T(8,128)} async-done(((f32[512,512]{0,1:T(8,128)}), f32[512,512]{0,1:T(8,128)}) %all-reduce.23.cloned.1.call-update) | async-done | bytes 1048592 | tf_op jit(solution)/shard_map/psum | solution.py:10
  937.7 20.8 %all-reduce.39.cloned.1.call-done = (f32[512,512]{1,0:T(8,128)}, f32[512,512]{0,1:T(8,128)}) async-done(((f32[512,512]{1,0:T(8,128)}, f32[512,512]{0,1:T(8,128)}), (f32[512,512]{1,0:T(8,128)}, f32[512,512]{0,1:T(8,128)})) %all-reduce.39.cloned.1.call-update) | async-done | bytes 2097168 | tf_op jit(solution)/shard_map/psum | solution.py:48
  958.7 73.5 %all-reduce.33.cloned.1.call-done = (f32[512,512]{1,0:T(8,128)}, f32[512,512]{0,1:T(8,128)}) async-done(((f32[512,512]{1,0:T(8,128)}, f32[512,512]{0,1:T(8,128)}), (f32[512,512]{1,0:T(8,128)}, f32[512,512]{0,1:T(8,128)})) %all-reduce.33.cloned.1.call-update) | async-done | bytes 2097168 | tf_op jit(solution)/shard_map/psum | solution.py:48
  1039.9 11.7 cholesky.534
  1064.1 12.2 cholesky.553
  1112.7 11.9 cholesky.591
  1140.2 39.3 %custom-call.42 = f32[4,128,128]{1,2,0:T(8,128)S(1)} custom-call(f32[4,128,128]{2,1,0:T(8,128)S(1)} %get-tuple-element.34), custom_call_target="InvertDiagBlocksLowerTriangular" | custom-call | tf_op jit(solution)/shard_map/jit(_solve_triangular)/triangular_solve | solution.py:40
  1192.7 49.1 %all-reduce.25.cloned.1.call-done = f32[512,512]{0,1:T(8,128)} async-done(((f32[512,512]{0,1:T(8,128)}), f32[512,512]{0,1:T(8,128)}) %all-reduce.25.cloned.1.call-update) | async-done | bytes 1048592 | tf_op jit(solution)/shard_map/psum | solution.py:10
  1245.9 20.8 %all-reduce.37.cloned.1.call-done = (f32[512,512]{1,0:T(8,128)}, f32[512,512]{0,1:T(8,128)}) async-done(((f32[512,512]{1,0:T(8,128)}, f32[512,512]{0,1:T(8,128)}), (f32[512,512]{1,0:T(8,128)}, f32[512,512]{0,1:T(8,128)})) %all-reduce.37.cloned.1.call-update) | async-done | bytes 2097168 | tf_op jit(solution)/shard_map/psum | solution.py:48
  1267.2 73.2 %all-reduce.31.cloned.1.call-done = (f32[512,512]{1,0:T(8,128)}, f32[512,512]{0,1:T(8,128)}) async-done(((f32[512,512]{1,0:T(8,128)}, f32[512,512]{0,1:T(8,128)}), (f32[512,512]{1,0:T(8,128)}, f32[512,512]{0,1:T(8,128)})) %all-reduce.31.cloned.1.call-update) | async-done | bytes 2097168 | tf_op jit(solution)/shard_map/psum | solution.py:48
  1372.2 11.9 cholesky.625
  1420.5 12.1 cholesky.663
  1448.3 39.3 %custom-call.46 = f32[4,128,128]{1,2,0:T(8,128)S(1)} custom-call(f32[4,128,128]{2,1,0:T(8,128)S(1)} %get-tuple-element.35), custom_call_target="InvertDiagBlocksLowerTriangular" | custom-call | tf_op jit(solution)/shard_map/jit(_solve_triangular)/triangular_solve | solution.py:40
  1500.7 49.1 %all-reduce.27.cloned.1.call-done = f32[512,512]{0,1:T(8,128)} async-done(((f32[512,512]{0,1:T(8,128)}), f32[512,512]{0,1:T(8,128)}) %all-reduce.27.cloned.1.call-update) | async-done | bytes 1048592 | tf_op jit(solution)/shard_map/psum | solution.py:10
  1554.1 20.6 %all-reduce.35.cloned.1.call-done = (f32[512,512]{1,0:T(8,128)}, f32[512,512]{0,1:T(8,128)}) async-done(((f32[512,512]{1,0:T(8,128)}, f32[512,512]{0,1:T(8,128)}), (f32[512,512]{1,0:T(8,128)}, f32[512,512]{0,1:T(8,128)})) %all-reduce.35.cloned.1.call-update) | async-done | bytes 2097168 | tf_op jit(solution)/shard_map/psum | solution.py:48
  1574.8 73.6 %all-reduce.29.cloned.1.call-done = (f32[512,512]{1,0:T(8,128)}, f32[512,512]{0,1:T(8,128)}) async-done(((f32[512,512]{1,0:T(8,128)}, f32[512,512]{0,1:T(8,128)}), (f32[512,512]{1,0:T(8,128)}, f32[512,512]{0,1:T(8,128)})) %all-reduce.29.cloned.1.call-update) | async-done | bytes 2097168 | tf_op jit(solution)/shard_map/psum | solution.py:48
  1681.9 11.9 cholesky.697
  1733.0 11.9 cholesky.735
  1751.9 13.5 while.11
  1765.4 40.1 %custom-call.50 = f32[4,128,128]{1,2,0:T(8,128)S(1)} custom-call(f32[4,128,128]{2,1,0:T(8,128)} %get-tuple-element.36), custom_call_target="InvertDiagBlocksLowerTriangular" | custom-call | tf_op jit(solution)/shard_map/jit(_solve_triangular)/triangular_solve | solution.py:40
  (254 shorter events, 403.3 us)
Async XLA Ops:
  6.5 588.5 %copy-start = (f32[512,512]{1,0:T(8,128)S(1)}, f32[512,512]{1,0:T(8,128)}, u32[]{:S(2)}) copy-start(f32[512,512]{1,0:T(8,128)} %param.6) | copy-start | bytes 3145732
  6.5 93.6 %all-gather.3.cloned.1.call-start = ((), (), s32[]{:S(2)}) async-start(), calls=%async_computation.2 | async-start | bytes 10485760 | tf_op jit(solution)/shard_map/all_gather | solution.py:65
  9.8 389.6 %all-reduce.19.cloned.1.call-start = ((), (), s32[]{:S(2)}) async-start(), calls=%async_computation.3 | async-start | bytes 16777216 | tf_op jit(solution)/shard_map/psum | solution.py:10
  108.4 334.3 %reduce-scatter.3.cloned.1.call-start = ((), (), s32[]{:S(2)}) async-start(), calls=%async_computation.4 | async-start | bytes 6291456 | tf_op jit(solution)/shard_map/reduce_scatter | solution.py:67
  431.5 163.5 %all-gather.5.cloned.1.call-start = ((), (), s32[]{:S(2)}) async-start(), calls=%async_computation.5 | async-start | bytes 10485760 | tf_op jit(solution)/shard_map/all_gather | solution.py:79
  442.7 239.1 %reduce-scatter.5.cloned.1.call-start = ((), (), s32[]{:S(2)}) async-start(), calls=%async_computation.6 | async-start | bytes 9437184 | tf_op jit(solution)/shard_map/reduce_scatter | solution.py:28
  612.2 131.0 %all-reduce.21.cloned.1.call-start = ((), (), s32[]{:S(2)}) async-start(), calls=%async_computation.7 | async-start | bytes 2097152 | tf_op jit(solution)/shard_map/psum | solution.py:37
  681.8 196.0 %copy-start.2 = (f32[512,512]{0,1:T(8,128)S(1)}, f32[512,512]{0,1:T(8,128)}, u32[]{:S(2)}) copy-start(f32[512,512]{0,1:T(8,128)} %reduce-scatter.5.cloned.1.call-done) | copy-start | bytes 3145732
  686.3 247.2 %all-reduce.23.cloned.1.call-start = ((), (), s32[]{:S(2)}) async-start(), calls=%async_computation.8 | async-start | bytes 2097152 | tf_op jit(solution)/shard_map/psum | solution.py:10
  882.2 76.2 %all-reduce.39.cloned.1.call-start = ((), (), s32[]{:S(2)}) async-start(), calls=%async_computation.16 | async-start | bytes 4194304 | tf_op jit(solution)/shard_map/psum | solution.py:48
  937.6 94.6 %all-reduce.33.cloned.1.call-start = ((), (), s32[]{:S(2)}) async-start(), calls=%async_computation.13 | async-start | bytes 4194304 | tf_op jit(solution)/shard_map/psum | solution.py:48
  958.4 283.3 %all-reduce.25.cloned.1.call-start = ((), (), s32[]{:S(2)}) async-start(), calls=%async_computation.9 | async-start | bytes 2097152 | tf_op jit(solution)/shard_map/psum | solution.py:10
  1032.2 147.3 %copy-start.4 = (f32[512,512]{1,0:T(8,128)S(1)}, f32[512,512]{1,0:T(8,128)}, u32[]{:S(2)}) copy-start(f32[512,512]{1,0:T(8,128)} %get-tuple-element.73) | copy-start | bytes 3145732
  1038.9 1.0 copy-start.6
  1189.7 76.9 %all-reduce.37.cloned.1.call-start = ((), (), s32[]{:S(2)}) async-start(), calls=%async_computation.15 | async-start | bytes 4194304 | tf_op jit(solution)/shard_map/psum | solution.py:48
  1245.9 94.5 %all-reduce.31.cloned.1.call-start = ((), (), s32[]{:S(2)}) async-start(), calls=%async_computation.12 | async-start | bytes 4194304 | tf_op jit(solution)/shard_map/psum | solution.py:48
  1266.7 283.1 %all-reduce.27.cloned.1.call-start = ((), (), s32[]{:S(2)}) async-start(), calls=%async_computation.10 | async-start | bytes 2097152 | tf_op jit(solution)/shard_map/psum | solution.py:10
  1340.3 147.3 %copy-start.5 = (f32[512,512]{1,0:T(8,128)S(1)}, f32[512,512]{1,0:T(8,128)}, u32[]{:S(2)}) copy-start(f32[512,512]{1,0:T(8,128)} %get-tuple-element.71) | copy-start | bytes 3145732
  1347.0 1.0 copy-start.7
  1497.8 76.9 %all-reduce.35.cloned.1.call-start = ((), (), s32[]{:S(2)}) async-start(), calls=%async_computation.14 | async-start | bytes 4194304 | tf_op jit(solution)/shard_map/psum | solution.py:48
  1553.9 94.4 %all-reduce.29.cloned.1.call-start = ((), (), s32[]{:S(2)}) async-start(), calls=%async_computation.11 | async-start | bytes 4194304 | tf_op jit(solution)/shard_map/psum | solution.py:48
  1648.4 157.2 %copy-start.3 = (f32[512,512]{1,0:T(8,128)S(1)}, f32[512,512]{1,0:T(8,128)}, u32[]{:S(2)}) copy-start(f32[512,512]{1,0:T(8,128)} %get-tuple-element.69) | copy-start | bytes 3145732
  1655.1 1.0 copy-start.8
  1748.7 67.4 %copy-start.1 = (f32[512,512]{1,0:T(8,128)S(1)}, f32[512,512]{1,0:T(8,128)}, u32[]{:S(2)}) copy-start(f32[512,512]{1,0:T(8,128)} %param.6) | copy-start | bytes 3145732
Sparse Core Ops, SparseCore 0:
  9.9 90.1 all-gather.2
  108.5 290.8 all-reduce.18
  431.7 10.9 reduce-scatter.2
  444.1 150.8 all-gather.4
  612.3 69.4 reduce-scatter.4
  686.5 56.7 all-reduce.20
  882.4 51.1 all-reduce.22
  937.7 20.6 all-reduce.38
  961.5 70.6 all-reduce.32
  1189.9 51.8 all-reduce.24
  1246.0 20.6 all-reduce.36
  1269.6 70.6 all-reduce.30
  1497.9 51.8 all-reduce.26
  1554.0 20.6 all-reduce.34
  1577.7 70.6 all-reduce.28
